TPU v7x, 32 devices: a whole 2x2x4 slice. The times are simulated.
32 devices in a mesh: grp: 4 (over x, core), dev: 8 (over z, y).
Axes of the slice: x: 2, y: 2, z: 4, core: 2. Of those that a mesh axis runs over, the one named last changes fastest.
Arguments:
- sep_inv: bfloat16 [4096, 4096], P('grp', 'dev'), may hold values from -0.125 to 0.125
- panels: bfloat16 [4, 48, 2048, 128], P('grp', 'dev'), may hold values from -1.1953125 to 1.1953125
- diag_inverse: bfloat16 [4, 48, 768, 128], P('grp', 'dev'), may hold values from -6 to 6
- widths: int32 [4, 16], P('grp'), may hold values from 1 to 6, 48 in all within a row
- ancestors: int32 [4, 16, 16], P('grp'), may hold values from 0 to 31, as said below
Outputs:
- off_diag: bfloat16 [4, 48, 2048, 128], P('grp', 'dev')
- diag_panels: bfloat16 [4, 48, 768, 128], P('grp', 'dev')
Inputs may be any that keep to these rules, and one draw needn't show every extreme that they name: `widths`: each row of a subtree sums to 48. `ancestors`: each supernode's list holds 16 different separator tile numbers in increasing order.
All inputs are finite; a program needn't handle non-finite values.
Results may differ from a plain program's by a relative error of at most 0.0046.
Values may be sent and summed in bfloat16 or wider, within the bound.
A program may use at most 320 MiB of HBM per device.

v0:
```python
import jax
import jax.numpy as jnp
from jax import lax
from jax.sharding import PartitionSpec as P


def extended_2(cells, sides, width):
    for axis, dim in sides:
        count = lax.axis_size(axis)
        ends = count - 1
        head = lax.slice_in_dim(cells, 0, width, axis=dim)
        tail = lax.slice_in_dim(cells, cells.shape[dim] - width, cells.shape[dim], axis=dim)
        cells = jnp.concatenate(
            [
                lax.ppermute(tail, axis, [(i, (i + 1) % count) for i in range(ends)]),
                cells,
                lax.ppermute(head, axis, [((i + 1) % count, i) for i in range(ends)]),
            ],
            axis=dim,
        )
    return cells


def on_device(sep_inv, panels, diag_inverse, widths, ancestors):
    group_count = lax.axis_size("grp")
    device_count = lax.axis_size("dev")
    rows_local = sep_inv.shape[0]
    cols_local = sep_inv.shape[1]
    stacked = lax.all_gather(sep_inv[None], ("grp", "dev"), axis=0, tiled=True)
    whole_sep = stacked.reshape(group_count, device_count, rows_local, cols_local)
    whole_sep = whole_sep.transpose(0, 2, 1, 3).reshape(
        group_count * rows_local, device_count * cols_local
    )
    block = panels.shape[3]
    anc_rows = panels.shape[2]
    anc_tiles = anc_rows // block
    local_units = panels.shape[1]
    max_tiles = diag_inverse.shape[2] // block
    sep_order = whole_sep.shape[0]
    count_blocks = sep_order // block
    row_tiles = whole_sep.reshape(count_blocks, block, sep_order)
    extended = extended_2(panels, (("dev", 1),), max_tiles - 1)
    width_row = widths[0]
    anc_table = ancestors[0]
    supernodes = width_row.shape[0]
    ends = jnp.cumsum(width_row)
    starts = ends - width_row
    position = lax.axis_index("dev") * local_units + jnp.arange(local_units, dtype=jnp.int32)
    owner = jnp.sum((ends[None, :] <= position[:, None]).astype(jnp.int32), axis=1)
    one_hot = (jnp.arange(supernodes, dtype=jnp.int32)[None, :] == owner[:, None]).astype(jnp.int32)
    column = position - jnp.sum(one_hot * starts[None, :], axis=1)
    width_unit = jnp.sum(one_hot * width_row[None, :], axis=1)
    blocks = jnp.sum(one_hot[:, :, None] * anc_table[None, :, :], axis=1)
    tile_ids = jnp.arange(count_blocks, dtype=jnp.int32)

    def per_unit(unit_idx):
        chosen = blocks[unit_idx]
        rows_pick = jnp.take(row_tiles, chosen, axis=0).reshape(anc_rows, sep_order)
        placing = (tile_ids[:, None] == chosen[None, :]).astype(jnp.bfloat16)
        panel_flat = panels[0, unit_idx].reshape(anc_tiles, block * block)
        spread = jnp.dot(placing, panel_flat, preferred_element_type=jnp.float32)
        spread = spread.astype(jnp.bfloat16).reshape(sep_order, block)
        product = jnp.dot(rows_pick, spread, preferred_element_type=jnp.float32)
        result_x = (-product).astype(jnp.bfloat16)
        start_at = unit_idx + max_tiles - 1 - column[unit_idx]
        related = lax.dynamic_slice_in_dim(extended[0], start_at, max_tiles, 0)
        inner = jnp.einsum("jrb,rc->jbc", related, result_x, preferred_element_type=jnp.float32)
        keep = (jnp.arange(max_tiles, dtype=jnp.int32) < width_unit[unit_idx]).astype(jnp.float32)
        diag_block = (
            diag_inverse[0, unit_idx].astype(jnp.float32).reshape(max_tiles, block, block) - inner
        ) * keep[:, None, None]
        return (result_x, diag_block.reshape(max_tiles * block, block).astype(jnp.bfloat16))

    off_diag, diag_panels = lax.map(per_unit, jnp.arange(local_units, dtype=jnp.int32))
    return (off_diag[None], diag_panels[None])


def solution(mesh):
    placed = (
        P("grp", "dev"),
        P("grp", "dev", None, None),
        P("grp", "dev", None, None),
        P("grp", None),
        P("grp", None, None),
    )
    return jax.shard_map(
        on_device,
        mesh=mesh,
        in_specs=placed,
        out_specs=(P("grp", "dev", None, None), P("grp", "dev", None, None)),
        check_vma=False,
    )
```

profile of v0, /device:TPU:0, one launch (start us, length us, event | category | flops | bytes accessed | tf_op | source)
XLA Modules:
  0.0 590.8 jit_solution(17755719761780135666)
XLA Ops:
  7.9 3.2 copy.19
  11.1 3.0 fusion.24
  14.1 6.4 %collective-permute-start = (bf16[1,5,2048,128]{2,3,1,0:T(8,128)(2,1)}, bf16[1,5,2048,128]{2,3,1,0:T(8,128)(2,1)}, u32[]{:S(2)}, u32[]{:S(2)}) collective-permute-start(bf16[1,5,2048,128]{2,3,1,0:T(8,128)(2,1)} %get-tuple-element.293), channel_id=1, source_target_pairs={{0,1},{1,2},{2,3},{3,4},{4,5},{5,6},{6,7},{8,9},{9,10},{10,11},{11... | collective-permute-start | bytes 7864328 | tf_op jit(solution)/shard_map/ppermute | solution.py:15
  20.5 1.3 collective-permute-start.1
  22.7 131.4 %collective-permute-done = bf16[1,5,2048,128]{2,3,1,0:T(8,128)(2,1)} collective-permute-done((bf16[1,5,2048,128]{2,3,1,0:T(8,128)(2,1)}, bf16[1,5,2048,128]{2,3,1,0:T(8,128)(2,1)}, u32[]{:S(2)}, u32[]{:S(2)}) %collective-permute-start) | collective-permute-done | bytes 2621472 | tf_op jit(solution)/shard_map/ppermute | solution.py:15
  154.1 6.3 %pad_maximum_fusion = bf16[1,16,2048,128]{2,3,1,0:T(8,128)(2,1)} fusion(bf16[1,5,2048,128]{2,3,1,0:T(8,128)(2,1)} %collective-permute-done.1, bf16[1,6,2048,128]{2,3,1,0:T(8,128)(2,1)S(1)} %copy.19, bf16[1,5,2048,128]{2,3,1,0:T(8,128)(2,1)} %collective-permute-done), kind=kLoop, calls=%fused_computation.29 | loop fusion | flops 8388608 | bytes 16777216 | tf_op jit(solution)/shard_map/concatenate | solution.py:13
  160.5 110.9 %all-gather.3.cloned.1.call-done = bf16[32768,512]{1,0:T(8,128)(2,1)} async-done(((bf16[1024,512]{1,0:T(8,128)(2,1)}), bf16[32768,512]{1,0:T(8,128)(2,1)}) %all-gather.3.cloned.1.call-update) | async-done | bytes 33554448 | tf_op jit(solution)/shard_map/all_gather | solution.py:29
  271.3 31.1 %copy.23 = bf16[4,8,1024,512]{3,1,2,0:T(8,128)(2,1)} copy(bf16[4,8,1024,512]{3,2,1,0:T(8,128)(2,1)} %bitcast.82) | data formatting | bytes 67108864 | tf_op jit(solution)/shard_map/reshape | solution.py:30
  302.5 49.9 %reshape_reshape.3 = bf16[32,128,4096]{2,1,0:T(8,128)(2,1)} reshape(bf16[4,1024,8,512]{3,2,1,0:T(8,128)(2,1)} %bitcast.81) | data formatting | bytes 67108864 | tf_op jit(solution)/shard_map/reshape;reshape | solution.py:41
  352.3 231.6 %while.17 = (s32[]{:T(128)}, bf16[6,2048,128]{2,1,0:T(8,128)(2,1)}, bf16[6,768,128]{2,1,0:T(8,128)(2,1)}, s32[6]{0:T(128)S(1)}, s32[6,16]{1,0:T(8,128)S(1)}, /*i...) while((s32[]{:T(128)}, bf16[6,2048,128]{2,1,0:T(8,128)(2,1)}, ...), condition=%wide.region_6.7_spmd.clone, body=%wide.region_5.6_spmd.clone.sunk | while | flops 2576746240 | bytes 96605016 | solution.py:74
  358.4 0.9 constant_dynamic-slice_fusion.6
  359.4 1.1 constant_dynamic-slice_fusion.5
  361.6 11.8 %gather_fusion = bf16[16,128,4096]{2,1,0:T(8,128)(2,1)} fusion(bf16[32,128,4096]{2,1,0:T(8,128)(2,1)} %get-tuple-element.407, s32[1024]{0:T(1024)S(1)} %pad_clamp_fusion.2), kind=kCustom, calls=%fused_computation.clone.clone.1 | custom fusion | bytes 33554496 | tf_op jit(solution)/shard_map/while/body/eval_jaxpr/jit(_take)/gather | solution.py:58
  373.4 8.5 %broadcast_select_fusion.2 = bf16[16,128,4096]{2,1,0:T(8,128)(2,1)S(1)} fusion(bf16[16,128,4096]{2,1,0:T(8,128)(2,1)} %gather_fusion, pred[16]{0:T(512)(128)(4,1)S(1)} %get-tuple-element.366), kind=kLoop, calls=%fused_computation.3.clone.1 | loop fusion | flops 8388608 | bytes 33554448 | tf_op jit(solution)/shard_map/while/body/eval_jaxpr/jit(_take)/select_n | solution.py:58
  381.9 5.5 bitcast_dynamic-update-slice_fusion.4
  387.4 2.9 fusion.41
  390.3 0.7 bitcast_dynamic-update-slice_fusion.5
  397.0 0.9 constant_dynamic-slice_fusion.6
  398.0 1.1 constant_dynamic-slice_fusion.5
  400.2 11.8 %gather_fusion = bf16[16,128,4096]{2,1,0:T(8,128)(2,1)} fusion(bf16[32,128,4096]{2,1,0:T(8,128)(2,1)} %get-tuple-element.407, s32[1024]{0:T(1024)S(1)} %pad_clamp_fusion.2), kind=kCustom, calls=%fused_computation.clone.clone.1 | custom fusion | bytes 33554496 | tf_op jit(solution)/shard_map/while/body/eval_jaxpr/jit(_take)/gather | solution.py:58
  412.0 8.5 %broadcast_select_fusion.2 = bf16[16,128,4096]{2,1,0:T(8,128)(2,1)S(1)} fusion(bf16[16,128,4096]{2,1,0:T(8,128)(2,1)} %gather_fusion, pred[16]{0:T(512)(128)(4,1)S(1)} %get-tuple-element.366), kind=kLoop, calls=%fused_computation.3.clone.1 | loop fusion | flops 8388608 | bytes 33554448 | tf_op jit(solution)/shard_map/while/body/eval_jaxpr/jit(_take)/select_n | solution.py:58
  420.5 5.5 bitcast_dynamic-update-slice_fusion.4
  426.0 2.9 fusion.41
  428.9 0.7 bitcast_dynamic-update-slice_fusion.5
  435.6 0.9 constant_dynamic-slice_fusion.6
  436.6 1.1 constant_dynamic-slice_fusion.5
  438.8 11.8 %gather_fusion = bf16[16,128,4096]{2,1,0:T(8,128)(2,1)} fusion(bf16[32,128,4096]{2,1,0:T(8,128)(2,1)} %get-tuple-element.407, s32[1024]{0:T(1024)S(1)} %pad_clamp_fusion.2), kind=kCustom, calls=%fused_computation.clone.clone.1 | custom fusion | bytes 33554496 | tf_op jit(solution)/shard_map/while/body/eval_jaxpr/jit(_take)/gather | solution.py:58
  450.6 8.5 %broadcast_select_fusion.2 = bf16[16,128,4096]{2,1,0:T(8,128)(2,1)S(1)} fusion(bf16[16,128,4096]{2,1,0:T(8,128)(2,1)} %gather_fusion, pred[16]{0:T(512)(128)(4,1)S(1)} %get-tuple-element.366), kind=kLoop, calls=%fused_computation.3.clone.1 | loop fusion | flops 8388608 | bytes 33554448 | tf_op jit(solution)/shard_map/while/body/eval_jaxpr/jit(_take)/select_n | solution.py:58
  459.1 5.5 bitcast_dynamic-update-slice_fusion.4
  464.6 2.9 fusion.41
  474.2 0.9 constant_dynamic-slice_fusion.6
  475.2 1.1 constant_dynamic-slice_fusion.5
  477.4 11.8 %gather_fusion = bf16[16,128,4096]{2,1,0:T(8,128)(2,1)} fusion(bf16[32,128,4096]{2,1,0:T(8,128)(2,1)} %get-tuple-element.407, s32[1024]{0:T(1024)S(1)} %pad_clamp_fusion.2), kind=kCustom, calls=%fused_computation.clone.clone.1 | custom fusion | bytes 33554496 | tf_op jit(solution)/shard_map/while/body/eval_jaxpr/jit(_take)/gather | solution.py:58
  489.2 8.5 %broadcast_select_fusion.2 = bf16[16,128,4096]{2,1,0:T(8,128)(2,1)S(1)} fusion(bf16[16,128,4096]{2,1,0:T(8,128)(2,1)} %gather_fusion, pred[16]{0:T(512)(128)(4,1)S(1)} %get-tuple-element.366), kind=kLoop, calls=%fused_computation.3.clone.1 | loop fusion | flops 8388608 | bytes 33554448 | tf_op jit(solution)/shard_map/while/body/eval_jaxpr/jit(_take)/select_n | solution.py:58
  497.7 5.5 bitcast_dynamic-update-slice_fusion.4
  503.2 2.9 fusion.41
  512.8 0.9 constant_dynamic-slice_fusion.6
  513.8 1.1 constant_dynamic-slice_fusion.5
  516.0 11.8 %gather_fusion = bf16[16,128,4096]{2,1,0:T(8,128)(2,1)} fusion(bf16[32,128,4096]{2,1,0:T(8,128)(2,1)} %get-tuple-element.407, s32[1024]{0:T(1024)S(1)} %pad_clamp_fusion.2), kind=kCustom, calls=%fused_computation.clone.clone.1 | custom fusion | bytes 33554496 | tf_op jit(solution)/shard_map/while/body/eval_jaxpr/jit(_take)/gather | solution.py:58
  527.8 8.5 %broadcast_select_fusion.2 = bf16[16,128,4096]{2,1,0:T(8,128)(2,1)S(1)} fusion(bf16[16,128,4096]{2,1,0:T(8,128)(2,1)} %gather_fusion, pred[16]{0:T(512)(128)(4,1)S(1)} %get-tuple-element.366), kind=kLoop, calls=%fused_computation.3.clone.1 | loop fusion | flops 8388608 | bytes 33554448 | tf_op jit(solution)/shard_map/while/body/eval_jaxpr/jit(_take)/select_n | solution.py:58
  536.3 5.5 bitcast_dynamic-update-slice_fusion.4
  541.8 2.9 fusion.41
  551.4 0.9 constant_dynamic-slice_fusion.6
  552.3 1.1 constant_dynamic-slice_fusion.5
  554.6 11.8 %gather_fusion = bf16[16,128,4096]{2,1,0:T(8,128)(2,1)} fusion(bf16[32,128,4096]{2,1,0:T(8,128)(2,1)} %get-tuple-element.407, s32[1024]{0:T(1024)S(1)} %pad_clamp_fusion.2), kind=kCustom, calls=%fused_computation.clone.clone.1 | custom fusion | bytes 33554496 | tf_op jit(solution)/shard_map/while/body/eval_jaxpr/jit(_take)/gather | solution.py:58
  566.4 8.5 %broadcast_select_fusion.2 = bf16[16,128,4096]{2,1,0:T(8,128)(2,1)S(1)} fusion(bf16[16,128,4096]{2,1,0:T(8,128)(2,1)} %gather_fusion, pred[16]{0:T(512)(128)(4,1)S(1)} %get-tuple-element.366), kind=kLoop, calls=%fused_computation.3.clone.1 | loop fusion | flops 8388608 | bytes 33554448 | tf_op jit(solution)/shard_map/while/body/eval_jaxpr/jit(_take)/select_n | solution.py:58
  574.9 5.5 bitcast_dynamic-update-slice_fusion.4
  580.4 2.9 fusion.41
  (84 shorter events, 27.2 us)
Async XLA Ops:
  7.2 264.1 %all-gather.3.cloned.1.call-start = ((), (), s32[]{:S(2)}) async-start(), calls=%async_computation | async-start | bytes 34603008 | tf_op jit(solution)/shard_map/all_gather | solution.py:29
  11.1 10.7 %copy-start.1 = (s32[1,16]{1,0:T(1,128)S(1)}, s32[1,16]{1,0:T(1,128)}, u32[]{:S(2)}) copy-start(s32[1,16]{1,0:T(1,128)} %param.10) | copy-start | bytes 196
  11.1 11.4 %copy-start = (s32[1,16,16]{2,1,0:T(8,128)S(1)}, s32[1,16,16]{2,1,0:T(8,128)}, u32[]{:S(2)}) copy-start(s32[1,16,16]{2,1,0:T(8,128)} %param.11) | copy-start | bytes 3076
  14.1 140.0 %collective-permute-start = (bf16[1,5,2048,128]{2,3,1,0:T(8,128)(2,1)}, bf16[1,5,2048,128]{2,3,1,0:T(8,128)(2,1)}, u32[]{:S(2)}, u32[]{:S(2)}) collective-permute-start(bf16[1,5,2048,128]{2,3,1,0:T(8,128)(2,1)} %get-tuple-element.293), channel_id=1, source_target_pairs={{0,1},{1,2},{2,3},{3,4},{4,5},{5,6},{6,7},{8,9},{9,10},{10,11},{11... | collective-permute-start | bytes 7864328 | tf_op jit(solution)/shard_map/ppermute | solution.py:15
  20.5 133.6 %collective-permute-start.1 = (bf16[1,5,2048,128]{2,3,1,0:T(8,128)(2,1)}, bf16[1,5,2048,128]{2,3,1,0:T(8,128)(2,1)}, u32[]{:S(2)}, u32[]{:S(2)}) collective-permute-start(bf16[1,5,2048,128]{2,3,1,0:T(8,128)(2,1)} %get-tuple-element.294), channel_id=1, source_target_pairs={{1,0},{2,1},{3,2},{4,3},{5,4},{6,5},{7,6},{9,8},{10,9},{11,10},{12... | collective-permute-start | bytes 7864328 | tf_op jit(solution)/shard_map/ppermute | solution.py:17
Sparse Core Ops, SparseCore 0:
  10.9 260.3 all-gather.2
where the time goes:
time: 594 us; the launch traced here: 591 us
  waiting for transfers between devices  243 us (41%)
  local copies, waits for them, and re-layouts  190 us (32%)
  other arithmetic  62.3 us (10%)
  matrix products  52.5 us (9%)
  loops' own time  20.7 us (3%)
  between operations  14.1 us (2%)
  starting transfers between devices  7.75 us (1%)
    ppermute x1, waiting for transfers between devices, extended_2(): lax.ppermute(tail, axis, [(i, (i + 1) % count) for i in range(ends)])  131 us
    all_gather x1, waiting for transfers between devices, on_device(): stacked = lax.all_gather(sep_inv[None], ('grp', 'dev'), axis=0, tiled=True)  111 us
    gather x6, local copies, waits for them, and re-layouts, per_unit(): rows_pick = jnp.take(row_tiles, chosen, axis=0).reshape(anc_rows, sep_order)  70.6 us
    select_n x12, other arithmetic, per_unit(): rows_pick = jnp.take(row_tiles, chosen, axis=0).reshape(anc_rows, sep_order)  51.1 us
    another operation x1, local copies, waits for them, and re-layouts, on_device(): row_tiles = whole_sep.reshape(count_blocks, block, sep_order)  49.9 us
    dot_general x6, matrix products, per_unit(): product = jnp.dot(rows_pick, spread, preferred_element_type=jnp.float32)  32.8 us
    reshape x1, local copies, waits for them, and re-layouts, on_device(): stacked.reshape(group_count, device_count, rows_local, cols_local)  31.1 us
    another operation x1, loops' own time, on_device(): lax.map(per_unit, jnp.arange(local_units, dtype=jnp.int32))  20.7 us
  transfers between devices with their start and end apart: 3, of which 2 were waited for; matrix products, arithmetic and copies ran while one was open for 2% of the time, Pallas kernels for 0%

commit v1 on v0

v1 whole, which is shorter than its diff:
```python
import functools
import jax
import jax.numpy as jnp
from jax import lax
from jax.experimental import pallas as pl
from jax.experimental.pallas import tpu as pltpu
from jax.sharding import PartitionSpec as P

PIECES = 2


def halo_2(cells, width, axis):
    count = lax.axis_size(axis)
    ends = count - 1
    head = lax.slice_in_dim(cells, 0, width, axis=0)
    tail = lax.slice_in_dim(cells, cells.shape[0] - width, cells.shape[0], axis=0)
    before = lax.ppermute(tail, axis, [(i, (i + 1) % count) for i in range(ends)])
    after = lax.ppermute(head, axis, [((i + 1) % count, i) for i in range(ends)])
    return jnp.concatenate([before, cells, after], axis=0)


def spread_kernel(tiles, anc_tiles, block, where_ref, panel_ref, out_ref):
    unit = pl.program_id(0)
    for t in range(tiles):
        at = where_ref[unit, t]
        row = pl.multiple_of(jnp.minimum(at, anc_tiles - 1) * block, block)
        tile = panel_ref[pl.ds(row, block), :]
        out_ref[t * block : (t + 1) * block, :] = jnp.where(at < anc_tiles, tile, jnp.zeros_like(tile))


def product_kernel(parts, part_cols, sep_ref, spread_ref, out_ref):
    rows = jnp.concatenate([sep_ref[d] for d in range(parts)], axis=1)
    total = jnp.dot(rows, spread_ref[...], preferred_element_type=jnp.float32)
    out_ref[...] = (-total).astype(out_ref.dtype)


def result_kernel(
    anc_tiles, max_tiles, block, per_part, per_piece,
    chosen_ref, start_ref, width_ref, *refs
):
    pieces = refs[:PIECES]
    ext_ref, dinv_ref, off_ref, diag_ref = refs[PIECES:]
    unit = pl.program_id(0)
    for a in range(anc_tiles):
        tile = chosen_ref[unit, a]
        inside = lax.rem(tile, per_part)
        piece = lax.div(inside, per_piece)
        index = lax.div(tile, per_part) * per_piece + lax.rem(inside, per_piece)
        row = pl.multiple_of(index * block, block)
        value = pieces[0][pl.ds(row, block), :]
        for p in range(1, PIECES):
            value = jnp.where(piece == p, pieces[p][pl.ds(row, block), :], value)
        off_ref[a * block : (a + 1) * block, :] = value
    start = start_ref[unit]
    width = width_ref[unit]
    related = jnp.concatenate([ext_ref[start + j] for j in range(max_tiles)], axis=1)
    inner = lax.dot_general(
        off_ref[...], related, (((0,), (0,)), ((), ())), preferred_element_type=jnp.float32
    )
    for j in range(max_tiles):
        rows = slice(j * block, (j + 1) * block)
        value = dinv_ref[rows, :].astype(jnp.float32) - inner[:, rows].T
        diag_ref[rows, :] = jnp.where(j < width, value, jnp.zeros_like(value)).astype(diag_ref.dtype)


def on_device(sep_inv, panels, diag_inverse, widths, ancestors):
    group_count = lax.axis_size("grp")
    device_count = lax.axis_size("dev")
    rows_local, cols_local = sep_inv.shape
    local_units, anc_rows, block = panels.shape[1:]
    anc_tiles = anc_rows // block
    max_tiles = diag_inverse.shape[2] // block
    sep_order = group_count * rows_local
    count_blocks = sep_order // block
    columns = local_units * block
    piece_rows = rows_local // PIECES
    gathered = [
        lax.all_gather(
            lax.slice_in_dim(sep_inv, p * piece_rows, (p + 1) * piece_rows, axis=0),
            ("grp", "dev"), axis=0, tiled=False,
        ).reshape(group_count, device_count, piece_rows, cols_local)
        for p in range(PIECES)
    ]
    extended = halo_2(panels[0], max_tiles - 1, "dev")

    width_row = widths[0]
    anc_table = ancestors[0]
    supernodes = width_row.shape[0]
    ends = jnp.cumsum(width_row)
    starts = ends - width_row
    position = lax.axis_index("dev") * local_units + jnp.arange(local_units, dtype=jnp.int32)
    owner = jnp.sum((ends[None, :] <= position[:, None]).astype(jnp.int32), axis=1)
    one_hot = (jnp.arange(supernodes, dtype=jnp.int32)[None, :] == owner[:, None]).astype(jnp.int32)
    column = position - jnp.sum(one_hot * starts[None, :], axis=1)
    width_unit = jnp.sum(one_hot * width_row[None, :], axis=1)
    chosen = jnp.sum(one_hot[:, :, None] * anc_table[None, :, :], axis=1)
    start_at = jnp.arange(local_units, dtype=jnp.int32) + (max_tiles - 1) - column
    tile_ids = jnp.arange(count_blocks, dtype=jnp.int32)
    hit = chosen[:, :, None] == tile_ids[None, None, :]
    slot = jnp.arange(anc_tiles, dtype=jnp.int32)[None, :, None]
    where_at = jnp.min(jnp.where(hit, slot, anc_tiles), axis=1).astype(jnp.int32)

    spread = pl.pallas_call(
        functools.partial(spread_kernel, count_blocks, anc_tiles, block),
        out_shape=jax.ShapeDtypeStruct((sep_order, columns), jnp.bfloat16),
        grid_spec=pltpu.PrefetchScalarGridSpec(
            num_scalar_prefetch=1,
            grid=(local_units,),
            in_specs=[pl.BlockSpec((None, anc_rows, block), lambda u, w: (u, 0, 0))],
            out_specs=pl.BlockSpec((sep_order, block), lambda u, w: (0, u)),
        ),
        cost_estimate=pl.CostEstimate(
            flops=sep_order * columns, transcendentals=0,
            bytes_accessed=4 * sep_order * columns,
        ),
        name="spread",
    )(where_at, panels[0])

    step_rows = min(256, piece_rows)
    steps = piece_rows // step_rows

    def product(piece):
        return pl.pallas_call(
            functools.partial(product_kernel, device_count, cols_local),
            out_shape=jax.ShapeDtypeStruct((group_count * piece_rows, columns), jnp.bfloat16),
            grid=(group_count, steps),
            in_specs=[
                pl.BlockSpec((None, device_count, step_rows, cols_local), lambda g, r: (g, 0, r, 0)),
                pl.BlockSpec((sep_order, columns), lambda g, r: (0, 0)),
            ],
            out_specs=pl.BlockSpec((step_rows, columns), lambda g, r: (g * steps + r, 0)),
            cost_estimate=pl.CostEstimate(
                flops=2 * group_count * piece_rows * sep_order * columns, transcendentals=0,
                bytes_accessed=2 * group_count * piece_rows * sep_order + 2 * sep_order * columns,
            ),
            name="product",
        )(piece, spread)

    products = [product(piece) for piece in gathered]
    piece_order = group_count * piece_rows
    off_diag, diag_panels = pl.pallas_call(
        functools.partial(
            result_kernel, anc_tiles, max_tiles, block, rows_local // block, piece_rows // block
        ),
        out_shape=(
            jax.ShapeDtypeStruct((local_units, anc_rows, block), jnp.bfloat16),
            jax.ShapeDtypeStruct((local_units, max_tiles * block, block), jnp.bfloat16),
        ),
        grid_spec=pltpu.PrefetchScalarGridSpec(
            num_scalar_prefetch=3,
            grid=(local_units,),
            in_specs=[pl.BlockSpec((piece_order, block), lambda u, *_: (0, u))] * PIECES
            + [
                pl.BlockSpec(extended.shape, lambda u, *_: (0, 0, 0)),
                pl.BlockSpec((None, max_tiles * block, block), lambda u, *_: (u, 0, 0)),
            ],
            out_specs=[
                pl.BlockSpec((None, anc_rows, block), lambda u, *_: (u, 0, 0)),
                pl.BlockSpec((None, max_tiles * block, block), lambda u, *_: (u, 0, 0)),
            ],
        ),
        cost_estimate=pl.CostEstimate(
            flops=2 * local_units * anc_rows * block * block * max_tiles, transcendentals=0,
            bytes_accessed=4 * sep_order * columns,
        ),
        name="result",
    )(chosen, start_at, width_unit, *products, extended, diag_inverse[0])
    return (off_diag[None], diag_panels[None])


def solution(mesh):
    placed = (
        P("grp", "dev"),
        P("grp", "dev", None, None),
        P("grp", "dev", None, None),
        P("grp", None),
        P("grp", None, None),
    )
    return jax.shard_map(
        on_device,
        mesh=mesh,
        in_specs=placed,
        out_specs=(P("grp", "dev", None, None), P("grp", "dev", None, None)),
        check_vma=False,
    )
```

time: 594 us -> 351 us (0.59)
  local copies, waits for them, and re-layouts: 190 us -> 5.55 us
  Pallas kernels: 0 us -> 57.4 us
  other arithmetic: 62.3 us -> 8.74 us
  matrix products: 52.5 us -> 0 us
  loops' own time: 20.7 us -> 0 us
  waiting for transfers between devices: 243 us -> 256 us
    gather x6 -> x0, local copies, waits for them, and re-layouts: 70.6 us -> none  [per_unit(): rows_pick = jnp.take(row_tiles, chosen, axis=0).reshape(anc_rows, sep_order)]
    pallas_call x0 -> x4, Pallas kernels: none -> 57.4 us  [the longest x2 37.5 us: product(): pl.pallas_call(functools.partial(product_kernel, device_count, cols_local...]
    dot_general x18 -> x0, matrix products: 52.5 us -> none  [the longest x6 32.8 us: per_unit(): product = jnp.dot(rows_pick, spread, preferred_element_type=jnp.float32)]
    select_n x12 -> x0, other arithmetic: 51.1 us -> none  [per_unit(): rows_pick = jnp.take(row_tiles, chosen, axis=0).reshape(anc_rows, sep_order)]
    another operation x1 -> x0, local copies, waits for them, and re-layouts: 49.9 us -> none  [on_device(): row_tiles = whole_sep.reshape(count_blocks, block, sep_order)]
    reshape x8 -> x1, local copies, waits for them, and re-layouts: 34.4 us -> 0.08 us  [the longest x1 31.1 us: on_device(): stacked.reshape(group_count, device_count, rows_local, cols_local)]
    all_gather x1 -> x2, waiting for transfers between devices: 111 us -> 136 us  [on_device(): lax.all_gather(lax.slice_in_dim(sep_inv, p * piece_rows, (p + 1) * piece_...]
    dynamic_slice x30 -> x0, local copies, waits for them, and re-layouts: 23.9 us -> none  [the longest x6 6.49 us: per_unit(): panel_flat = panels[0, unit_idx].reshape(anc_tiles, block * block)]
  transfers between devices with their start and end apart: 3 -> 4, of which waited for: 2 -> 4; matrix products, arithmetic and copies ran while one was open for 2% -> 3% of each run, Pallas kernels for 0% -> 8%
where the time goes in v1:
time: 351 us; the launch traced here: 350 us
  waiting for transfers between devices  256 us (73%)
  Pallas kernels  57.4 us (16%)
  between operations  14.1 us (4%)
  other arithmetic  8.74 us (2%)
  starting transfers between devices  8.36 us (2%)
  local copies, waits for them, and re-layouts  5.55 us (2%)
    all_gather x2, waiting for transfers between devices, on_device(): lax.all_gather(lax.slice_in_dim(sep_inv, p * piece_rows, (p + 1) * piece_...  136 us
    ppermute x1, waiting for transfers between devices, halo_2(): lax.ppermute(tail, axis, [(i, (i + 1) % count) for i in range(ends)])  72.4 us
    ppermute x1, waiting for transfers between devices, halo_2(): lax.ppermute(head, axis, [((i + 1) % count, i) for i in range(ends)])  47.5 us
    pallas_call x2, Pallas kernels, product(): pl.pallas_call(functools.partial(product_kernel, device_count, cols_local...  37.5 us
    pallas_call x1, Pallas kernels, on_device(): pl.pallas_call(functools.partial(result_kernel, anc_tiles, max_tiles, blo...  12.3 us
    pallas_call x1, Pallas kernels, on_device(): pl.pallas_call(functools.partial(spread_kernel, count_blocks, anc_tiles,...  7.54 us
  transfers between devices with their start and end apart: 4, of which 4 were waited for; matrix products, arithmetic and copies ran while one was open for 3% of the time, Pallas kernels for 8%

profile of v1, /device:TPU:0, one launch (start us, length us, event | category | flops | bytes accessed | tf_op | source)
XLA Modules:
  0.0 350.4 jit_solution(11108251789424487635)
XLA Ops:
  7.2 0.0 copy-start
  7.2 0.0 all-gather.5.cloned.1.call-start
  7.2 2.4 fusion.2
  9.6 0.0 all-gather.5.cloned.1.call-update
  9.6 0.0 all-gather.7.cloned.1.call-start
  9.7 0.7 all-gather.7.cloned.1.call-update
  10.4 0.0 copy-done
  10.4 0.0 copy-start.4
  10.4 0.0 copy-start.3
  10.4 3.1 slice_bitcast_fusion.1
  13.5 1.3 collective-permute-start.1
  14.8 7.0 %collective-permute-start = (bf16[5,2048,128]{2,1,0:T(8,128)(2,1)}, bf16[5,2048,128]{2,1,0:T(8,128)(2,1)}, u32[]{:S(2)}, u32[]{:S(2)}) collective-permute-start(bf16[5,2048,128]{2,1,0:T(8,128)(2,1)} %get-tuple-element.8), channel_id=1, source_target_pairs={{0,1},{1,2},{2,3},{3,4},{4,5},{5,6},{6,7},{8,9},{9,10},{10,11},{11... | collective-permute-start | bytes 7864328 | tf_op jit(solution)/shard_map/ppermute | solution.py:17
  21.8 0.0 copy-done.4
  21.8 0.1 copy.9
  21.9 0.1 reduce
  22.0 0.2 convert_reduce_fusion
  22.2 0.1 fusion
  22.3 0.0 copy-done.3
  22.3 0.1 multiply_reduce_fusion.chosen_ref
  22.4 0.0 copy-start.2
  22.4 0.7 select_reduce_fusion.where_ref
  23.1 0.0 copy-start.1
  23.1 7.5 %spread.1.spread_ref = bf16[4096,768]{1,0:T(8,128)(2,1)} custom-call(s32[6,32]{1,0:T(8,128)} %select_reduce_fusion.where_ref, bf16[6,2048,128]{2,1,0:T(8,128)(2,1)} %bitcast.19), custom_call_target="tpu_custom_call" | custom-call | flops 3145728 | bytes 12582912 | tf_op jit(solution)/shard_map/spread/pallas_call | solution.py:103
  30.6 0.0 copy-done.2
  30.6 0.7 select_reduce_fusion.1
  31.3 0.5 subtract_subtract_fusion.start_ref
  31.8 47.5 %collective-permute-done.1 = bf16[5,2048,128]{2,1,0:T(8,128)(2,1)} collective-permute-done((bf16[5,2048,128]{2,1,0:T(8,128)(2,1)}, bf16[5,2048,128]{2,1,0:T(8,128)(2,1)}, u32[]{:S(2)}, u32[]{:S(2)}) %collective-permute-start.1) | collective-permute-done | bytes 2621472 | tf_op jit(solution)/shard_map/ppermute | solution.py:18
  79.3 72.4 %collective-permute-done = bf16[5,2048,128]{2,1,0:T(8,128)(2,1)} collective-permute-done((bf16[5,2048,128]{2,1,0:T(8,128)(2,1)}, bf16[5,2048,128]{2,1,0:T(8,128)(2,1)}, u32[]{:S(2)}, u32[]{:S(2)}) %collective-permute-start) | collective-permute-done | bytes 2621472 | tf_op jit(solution)/shard_map/ppermute | solution.py:17
  151.7 0.0 copy-done.1
  151.7 6.3 %pad_maximum_fusion.refs_2_ = bf16[16,2048,128]{2,1,0:T(8,128)(2,1)} fusion(bf16[5,2048,128]{2,1,0:T(8,128)(2,1)} %collective-permute-done.1, bf16[6,2048,128]{2,1,0:T(8,128)(2,1)S(1)} %bitcast.20, bf16[5,2048,128]{2,1,0:T(8,128)(2,1)} %collective-permute-done), kind=kLoop, calls=%fused_computation | loop fusion | flops 8388608 | bytes 16777216 | tf_op jit(solution)/shard_map/concatenate | solution.py:19
  158.0 36.4 %all-gather.5.cloned.1.call-done = bf16[16384,512]{1,0:T(8,128)(2,1)} async-done(((bf16[512,512]{1,0:T(8,128)(2,1)}), bf16[16384,512]{1,0:T(8,128)(2,1)}) %all-gather.5.cloned.1.call-update) | async-done | bytes 16777232 | tf_op jit(solution)/shard_map/all_gather | solution.py:78
  194.4 18.8 %product.2.refs_0_ = bf16[2048,768]{1,0:T(8,128)(2,1)} custom-call(bf16[4,8,512,512]{3,2,1,0:T(8,128)(2,1)} %bitcast.25, bf16[4096,768]{1,0:T(8,128)(2,1)} %spread.1.spread_ref), custom_call_target="tpu_custom_call" | custom-call | flops 12884901888 | bytes 23068672 | tf_op jit(solution)/shard_map/product/pallas_call | solution.py:123
  213.2 99.3 %all-gather.7.cloned.1.call-done = bf16[16384,512]{1,0:T(8,128)(2,1)} async-done(((bf16[512,512]{1,0:T(8,128)(2,1)}), bf16[16384,512]{1,0:T(8,128)(2,1)}) %all-gather.7.cloned.1.call-update) | async-done | bytes 16777232 | tf_op jit(solution)/shard_map/all_gather | solution.py:78
  312.5 18.7 %product.3.refs_1_ = bf16[2048,768]{1,0:T(8,128)(2,1)} custom-call(bf16[4,8,512,512]{3,2,1,0:T(8,128)(2,1)} %bitcast.26, bf16[4096,768]{1,0:T(8,128)(2,1)} %spread.1.spread_ref), custom_call_target="tpu_custom_call" | custom-call | flops 12884901888 | bytes 23068672 | tf_op jit(solution)/shard_map/product/pallas_call | solution.py:123
  331.3 12.3 %result.1 = (bf16[6,2048,128]{2,1,0:T(8,128)(2,1)}, bf16[6,768,128]{2,1,0:T(8,128)(2,1)}) custom-call(s32[6,16]{1,0:T(8,128)} %copy-done.2, s32[6]{0:T(128)} %subtract_subtract_fusion.start_ref, s32[6]{0:T(128)} %get-tuple-element.6.width_ref, bf16[2048,768]{1,0:T(8,128)(2,1)} %product.2.refs_0_, bf16[2048,768]{1,0:T(8,128)(2,1)} %product.3.refs_1_, ...), custom_call_target="tpu_custom_call" | custom-call | flops 2415919104 | bytes 12582912 | tf_op jit(solution)/shard_map/result/pallas_call | solution.py:141
  (3 shorter events, 0.0 us)
Async XLA Ops:
  7.2 3.2 copy-start
  7.2 187.2 %all-gather.5.cloned.1.call-start = ((), (), s32[]{:S(2)}) async-start(), calls=%async_computation | async-start | bytes 17301504 | tf_op jit(solution)/shard_map/all_gather | solution.py:78
  9.6 302.9 %all-gather.7.cloned.1.call-start = ((), (), s32[]{:S(2)}) async-start(), calls=%async_computation.1 | async-start | bytes 17301504 | tf_op jit(solution)/shard_map/all_gather | solution.py:78
  10.4 11.4 %copy-start.4 = (s32[1,16]{1,0:T(1,128)S(1)}, s32[1,16]{1,0:T(1,128)}, u32[]{:S(2)}) copy-start(s32[1,16]{1,0:T(1,128)} %param.8) | copy-start | bytes 196
  10.4 11.9 %copy-start.3 = (s32[1,16,16]{2,1,0:T(8,128)S(1)}, s32[1,16,16]{2,1,0:T(8,128)}, u32[]{:S(2)}) copy-start(s32[1,16,16]{2,1,0:T(8,128)} %param.9) | copy-start | bytes 3076
  13.5 65.8 %collective-permute-start.1 = (bf16[5,2048,128]{2,1,0:T(8,128)(2,1)}, bf16[5,2048,128]{2,1,0:T(8,128)(2,1)}, u32[]{:S(2)}, u32[]{:S(2)}) collective-permute-start(bf16[5,2048,128]{2,1,0:T(8,128)(2,1)} %get-tuple-element.9), channel_id=1, source_target_pairs={{1,0},{2,1},{3,2},{4,3},{5,4},{6,5},{7,6},{9,8},{10,9},{11,10},{12... | collective-permute-start | bytes 7864328 | tf_op jit(solution)/shard_map/ppermute | solution.py:18
  14.8 136.9 %collective-permute-start = (bf16[5,2048,128]{2,1,0:T(8,128)(2,1)}, bf16[5,2048,128]{2,1,0:T(8,128)(2,1)}, u32[]{:S(2)}, u32[]{:S(2)}) collective-permute-start(bf16[5,2048,128]{2,1,0:T(8,128)(2,1)} %get-tuple-element.8), channel_id=1, source_target_pairs={{0,1},{1,2},{2,3},{3,4},{4,5},{5,6},{6,7},{8,9},{9,10},{10,11},{11... | collective-permute-start | bytes 7864328 | tf_op jit(solution)/shard_map/ppermute | solution.py:17
  22.4 8.2 %copy-start.2 = (s32[6,16]{1,0:T(8,128)}, s32[6,16]{1,0:T(8,128)S(1)}, u32[]{:S(2)}) copy-start(s32[6,16]{1,0:T(8,128)S(1)} %multiply_reduce_fusion.chosen_ref) | copy-start | bytes 1156
  23.1 128.6 %copy-start.1 = (bf16[1,6,2048,128]{3,2,1,0:T(8,128)(2,1)S(1)}, bf16[1,6,2048,128]{3,2,1,0:T(8,128)(2,1)}, u32[]{:S(2)}) copy-start(bf16[1,6,2048,128]{3,2,1,0:T(8,128)(2,1)} %param.6) | copy-start | bytes 9437188
Sparse Core Ops, SparseCore 0:
  11.1 183.3 all-gather.4
  198.1 114.4 all-gather.6
